TPU v7x, 8 devices: a whole 2x2x1 slice. The times are simulated.
8 devices in a mesh: data: 1 (over z), heads: 2 (over y), seq: 4 (over x, core).
Axes of the slice: x: 2, y: 2, z: 1, core: 2. Of those that a mesh axis runs over, the one named last changes fastest.
Arguments:
- tokens: bfloat16 [16, 768, 1024], P('data', 'seq')
- theta_q: bfloat16 [1024, 1024], P(None, 'heads')
- theta_k: bfloat16 [1024, 1024], P(None, 'heads')
- theta_v: bfloat16 [1024, 1024], P(None, 'heads')
- w_out: bfloat16 [1024, 1024], P('heads')
- w_one: float32 [16, 64, 256], P('heads')
- b_one: float32 [16, 256], P('heads')
- w_two: float32 [16, 256, 64], P('heads')
- b_two: float32 [16, 64], P('heads')
- ln_gain: float32 [16, 64], P('heads')
- ln_bias: float32 [16, 64], P('heads')
- inner_lr: float32 [16], P('heads')
Outputs:
- output: bfloat16 [16, 768, 1024], P('data', 'seq')
All inputs are finite; a program needn't handle non-finite values.
Results may differ from a plain program's by a relative error of at most 0.001.
Values are sent between devices in bfloat16 or wider.
A program may use at most 1 GiB of HBM per device.

v0:
```python
import jax
import jax.numpy as jnp
from jax import lax
from jax.sharding import PartitionSpec as P

MINI_BATCH = 16
LN_EPS = 1e-6
FULL_PREC = lax.Precision.HIGHEST


def layer_norm(z_out, ln_gain, ln_bias):
    row_mean = jnp.mean(z_out, axis=-1, keepdims=True)
    centered = z_out - row_mean
    inv_std = lax.rsqrt(jnp.mean(centered * centered, axis=-1, keepdims=True) + LN_EPS)
    normed = centered * inv_std
    return normed * ln_gain + ln_bias, normed, inv_std


def gelu_tanh(z_val):
    return jax.nn.gelu(z_val, approximate=True)


def inner_apply(inner_state, z_in, ln_gain, ln_bias):
    w_one, b_one, w_two, b_two = inner_state
    hidden = gelu_tanh(jnp.einsum('mgd,gdf->mgf', z_in, w_one, precision=FULL_PREC) + b_one)
    z_two = jnp.einsum('mgf,gfd->mgd', hidden, w_two, precision=FULL_PREC) + b_two
    return z_in + layer_norm(z_two, ln_gain, ln_bias)[0]


def inner_step(inner_state, block_set, ln_gain, ln_bias, step_lr):
    w_one, b_one, w_two, b_two = inner_state
    key_blk, query_blk, value_blk = block_set
    z_one = jnp.einsum('mgd,gdf->mgf', key_blk, w_one, precision=FULL_PREC) + b_one
    hidden, gelu_back = jax.vjp(gelu_tanh, z_one)
    z_two = jnp.einsum('mgf,gfd->mgd', hidden, w_two, precision=FULL_PREC) + b_two
    ln_out, normed, inv_std = layer_norm(z_two, ln_gain, ln_bias)
    d_out = 2.0 * (key_blk + ln_out - value_blk)
    d_norm = d_out * ln_gain
    d_two = inv_std * (d_norm - jnp.mean(d_norm, axis=-1, keepdims=True) - normed * jnp.mean(d_norm * normed, axis=-1, keepdims=True))
    g_w_two = jnp.einsum('mgf,mgd->gfd', hidden, d_two, precision=FULL_PREC)
    d_hidden = jnp.einsum('mgd,gfd->mgf', d_two, w_two, precision=FULL_PREC)
    d_one = gelu_back(d_hidden)[0]
    g_w_one = jnp.einsum('mgd,mgf->gdf', key_blk, d_one, precision=FULL_PREC)
    lr_mat = step_lr[:, None, None]
    lr_vec = step_lr[:, None]
    new_state = (w_one - lr_mat * g_w_one, b_one - lr_vec * jnp.sum(d_one, axis=0), w_two - lr_mat * g_w_two, b_two - lr_vec * jnp.sum(d_two, axis=0))
    return new_state, inner_apply(new_state, query_blk, ln_gain, ln_bias)


def solution(mesh):
    seq_size = mesh.shape['seq']
    shift_pairs = [(source, source + 1) for source in range(seq_size - 1)]

    def local_fn(tokens, theta_q, theta_k, theta_v, w_out, w_one, b_one, w_two, b_two, ln_gain, ln_bias, inner_lr):
        num_seqs, tok_local, model_dim = tokens.shape
        local_heads, head_dim, inner_dim = w_one.shape
        num_pairs = num_seqs * local_heads
        num_steps = tok_local // MINI_BATCH

        def project(weight_mat):
            projected = jnp.einsum('btd,dhe->tbhe', tokens, weight_mat.reshape(model_dim, local_heads, head_dim), preferred_element_type=jnp.float32)
            return projected.reshape(num_steps, MINI_BATCH, num_pairs, head_dim)

        block_sets = (project(theta_k), project(theta_q), project(theta_v))

        def per_pair(weight_arr):
            return jnp.broadcast_to(weight_arr, (num_seqs,) + weight_arr.shape).reshape((num_pairs,) + weight_arr.shape[1:])

        gain_pairs = per_pair(ln_gain)
        bias_pairs = per_pair(ln_bias)
        lr_pairs = per_pair(inner_lr / MINI_BATCH)
        init_state = tuple(per_pair(weight_arr) for weight_arr in (w_one, b_one, w_two, b_two))

        def scan_step(inner_state, block_set):
            return inner_step(inner_state, block_set, gain_pairs, bias_pairs, lr_pairs)

        def run_segment(inner_state, seg_outs):
            return lax.scan(scan_step, inner_state, block_sets)

        def keep_carry(inner_state, seg_outs):
            return inner_state, seg_outs

        my_pos = lax.axis_index('seq')
        zero_outs = jnp.zeros((num_steps, MINI_BATCH, num_pairs, head_dim), jnp.float32)

        def chain_turn(turn_idx, loop_carry):
            state_in, outs_in = loop_carry
            inner_state, seg_outs = lax.cond(my_pos == turn_idx, run_segment, keep_carry, state_in, outs_in)
            inner_state = tuple(lax.ppermute(state_piece, 'seq', shift_pairs) for state_piece in inner_state)
            return inner_state, seg_outs

        state_in, outs_in = lax.fori_loop(0, seq_size - 1, chain_turn, (init_state, zero_outs))
        final_state, seg_outs = lax.cond(my_pos == seq_size - 1, run_segment, keep_carry, state_in, outs_in)
        head_outs = seg_outs.astype(jnp.bfloat16).reshape(tok_local, num_seqs, local_heads, head_dim)
        part_out = jnp.einsum('tbhe,hed->btd', head_outs, w_out.reshape(local_heads, head_dim, model_dim), preferred_element_type=jnp.float32)
        return lax.psum(part_out, 'heads').astype(jnp.bfloat16)

    arg_specs = (P('data', 'seq', None), P(None, 'heads'), P(None, 'heads'), P(None, 'heads'), P('heads', None), P('heads', None, None), P('heads', None), P('heads', None, None), P('heads', None), P('heads', None), P('heads', None), P('heads'))
    return jax.shard_map(local_fn, mesh=mesh, in_specs=arg_specs, out_specs=P('data', 'seq', None), check_vma=False)
```

profile of v0, /device:TPU:3, one launch (start us, length us, event | category | flops | bytes accessed | tf_op | source)
XLA Modules:
  0.0 3727.0 jit_solution(4519672269955733149)
XLA Ops:
  11.1 12.2 copy.33
  23.3 17.8 copy.38
  51.3 12.3 copy.35
  63.6 17.8 copy.39
  91.5 12.5 copy.37
  104.0 17.8 copy.40
  135.6 2602.2 %while.67 = (s32[]{:T(128)}, f32[128,64,256]{2,1,0:T(8,128)}, f32[128,256]{1,0:T(8,128)}, f32[128,256,64]{1,2,0:T(8,128)}, f32[128,64]{1,0:T(8,128)}, /*index=5*...) while((s32[]{:T(128)}, f32[128,64,256]{2,1,0:T(8,128)}, ...), condition=%wide.region_13.14_spmd.clone, body=%wide.region_0.13_spmd.clone.sunk | while | flops 2856374272 | bytes 335442496 | solution.py:92
  151.0 22.4 collective-permute-done.3
  195.8 181.2 %collective-permute-done.3 = f32[128,64]{1,0:T(8,128)S(1)} collective-permute-done((f32[128,64]{1,0:T(8,128)}, f32[128,64]{1,0:T(8,128)S(1)}, u32[]{:S(2)}, u32[]{:S(2)}) %collective-permute-start.3) | collective-permute-done | bytes 32800 | tf_op jit(solution)/shard_map/while/body/eval_jaxpr/ppermute | solution.py:89
  399.1 2320.8 %collective-permute-done.3 = f32[128,64]{1,0:T(8,128)S(1)} collective-permute-done((f32[128,64]{1,0:T(8,128)}, f32[128,64]{1,0:T(8,128)S(1)}, u32[]{:S(2)}, u32[]{:S(2)}) %collective-permute-start.3) | collective-permute-done | bytes 32800 | tf_op jit(solution)/shard_map/while/body/eval_jaxpr/ppermute | solution.py:89
  2737.9 798.9 %conditional.2 = (bf16[12,16,128,64]{3,1,2,0:T(8,128)(2,1)}) conditional(s32[]{:T(128)} %convert_element_type.22, bf16[12,16,128,64]{3,1,2,0:T(8,128)(2,1)} %get-tuple-element.1397, (f32[8]{0:T(128)S(1)}, f32[12,16,128,64]{3,2,1,0:T(8,128)}, f32[8,64]{1,0:T(8,128)S(1)}, f32[8,64]{1,0:T(8,128)S(1)}, f32[12,16,128,64]{3,2,1,0:T(8,128)}, ...), branch_computations={%region_14.15_spmd, %region_15.26_spmd} | conditional | flops 2856374272 | bytes 234826304 | solution.py:93
  2738.5 792.8 %while.66 = (s32[]{:T(128)}, f32[128,64,256]{2,1,0:T(8,128)}, f32[128,256]{1,0:T(8,128)}, f32[128,256,64]{1,2,0:T(8,128)}, f32[128,64]{1,0:T(8,128)}, /*index=5*...) while((s32[]{:T(128)}, f32[128,64,256]{2,1,0:T(8,128)}, ...), condition=%wide.wide.region_25.25_spmd, body=%wide.wide.region_16.24_spmd.sunk | while | flops 2856374272 | bytes 234752896 | solution.py:78
  2856.4 9.8 multiply_subtract_fusion.30
  2921.7 9.8 multiply_subtract_fusion.30
  2987.0 9.8 multiply_subtract_fusion.30
  3052.3 9.8 multiply_subtract_fusion.30
  3117.5 9.8 multiply_subtract_fusion.30
  3182.8 9.8 multiply_subtract_fusion.30
  3248.1 9.8 multiply_subtract_fusion.30
  3313.4 9.8 multiply_subtract_fusion.30
  3378.7 9.8 multiply_subtract_fusion.30
  3444.0 9.8 multiply_subtract_fusion.30
  3509.3 9.8 multiply_subtract_fusion.30
  3560.5 157.2 %all-reduce.1 = bf16[16,192,1024]{2,0,1:T(8,128)(2,1)} all-reduce(f32[16,192,1024]{2,0,1:T(8,128)} %fusion.118), channel_id=1, replica_groups=mesh['data'=1,'heads'=2,'seq'=4] {'heads'}, use_global_device_ids=true, to_apply=%region_26.27 | all-reduce | flops 3145728 | bytes 18874368 | tf_op jit(solution)/shard_map/psum | solution.py:96
  (584 shorter events, 824.2 us)
Async XLA Ops:
  0.0 3551.4 %copy-start = (bf16[512,1024]{1,0:T(8,128)(2,1)S(1)}, bf16[512,1024]{1,0:T(8,128)(2,1)}, u32[]{:S(2)}) copy-start(bf16[512,1024]{1,0:T(8,128)(2,1)} %param.26) | copy-start | bytes 3145732
  23.3 17.8 copy-start.15
  63.6 17.8 copy-start.16
  104.0 17.8 copy-start.27
  104.0 17.8 copy-start.18
  145.8 28.8 collective-permute-start
  147.1 35.3 collective-permute-start.2
  148.4 25.6 collective-permute-start.1
  149.7 23.7 collective-permute-start.3
  190.6 187.7 %collective-permute-start = (f32[128,64,256]{2,1,0:T(8,128)}, f32[128,64,256]{2,1,0:T(8,128)}, u32[]{:S(2)}, u32[]{:S(2)}) collective-permute-start(f32[128,64,256]{2,1,0:T(8,128)} %get-tuple-element.1171), channel_id=1, source_target_pairs={{0,1},{1,2},{2,3},{4,5},{5,6},{6,7}} | collective-permute-start | bytes 25165832 | tf_op jit(solution)/shard_map/while/body/eval_jaxpr/ppermute | solution.py:89
  191.9 194.2 %collective-permute-start.2 = (f32[128,256,64]{1,2,0:T(8,128)}, f32[128,256,64]{1,2,0:T(8,128)}, u32[]{:S(2)}, u32[]{:S(2)}) collective-permute-start(f32[128,256,64]{1,2,0:T(8,128)} %get-tuple-element.1173), channel_id=1, source_target_pairs={{0,1},{1,2},{2,3},{4,5},{5,6},{6,7}} | collective-permute-start | bytes 25165832 | tf_op jit(solution)/shard_map/while/body/eval_jaxpr/ppermute | solution.py:89
  193.2 184.4 %collective-permute-start.1 = (f32[128,256]{1,0:T(8,128)}, f32[128,256]{1,0:T(8,128)S(1)}, u32[]{:S(2)}, u32[]{:S(2)}) collective-permute-start(f32[128,256]{1,0:T(8,128)} %get-tuple-element.1172), channel_id=1, source_target_pairs={{0,1},{1,2},{2,3},{4,5},{5,6},{6,7}} | collective-permute-start | bytes 393224 | tf_op jit(solution)/shard_map/while/body/eval_jaxpr/ppermute | solution.py:89
  194.5 182.5 %collective-permute-start.3 = (f32[128,64]{1,0:T(8,128)}, f32[128,64]{1,0:T(8,128)S(1)}, u32[]{:S(2)}, u32[]{:S(2)}) collective-permute-start(f32[128,64]{1,0:T(8,128)} %get-tuple-element.1174), channel_id=1, source_target_pairs={{0,1},{1,2},{2,3},{4,5},{5,6},{6,7}} | collective-permute-start | bytes 98312 | tf_op jit(solution)/shard_map/while/body/eval_jaxpr/ppermute | solution.py:89
  393.9 2327.3 %collective-permute-start = (f32[128,64,256]{2,1,0:T(8,128)}, f32[128,64,256]{2,1,0:T(8,128)}, u32[]{:S(2)}, u32[]{:S(2)}) collective-permute-start(f32[128,64,256]{2,1,0:T(8,128)} %get-tuple-element.1171), channel_id=1, source_target_pairs={{0,1},{1,2},{2,3},{4,5},{5,6},{6,7}} | collective-permute-start | bytes 25165832 | tf_op jit(solution)/shard_map/while/body/eval_jaxpr/ppermute | solution.py:89
  395.2 2333.8 %collective-permute-start.2 = (f32[128,256,64]{1,2,0:T(8,128)}, f32[128,256,64]{1,2,0:T(8,128)}, u32[]{:S(2)}, u32[]{:S(2)}) collective-permute-start(f32[128,256,64]{1,2,0:T(8,128)} %get-tuple-element.1173), channel_id=1, source_target_pairs={{0,1},{1,2},{2,3},{4,5},{5,6},{6,7}} | collective-permute-start | bytes 25165832 | tf_op jit(solution)/shard_map/while/body/eval_jaxpr/ppermute | solution.py:89
  396.5 2324.0 %collective-permute-start.1 = (f32[128,256]{1,0:T(8,128)}, f32[128,256]{1,0:T(8,128)S(1)}, u32[]{:S(2)}, u32[]{:S(2)}) collective-permute-start(f32[128,256]{1,0:T(8,128)} %get-tuple-element.1172), channel_id=1, source_target_pairs={{0,1},{1,2},{2,3},{4,5},{5,6},{6,7}} | collective-permute-start | bytes 393224 | tf_op jit(solution)/shard_map/while/body/eval_jaxpr/ppermute | solution.py:89
  397.8 2322.1 %collective-permute-start.3 = (f32[128,64]{1,0:T(8,128)}, f32[128,64]{1,0:T(8,128)S(1)}, u32[]{:S(2)}, u32[]{:S(2)}) collective-permute-start(f32[128,64]{1,0:T(8,128)} %get-tuple-element.1174), channel_id=1, source_target_pairs={{0,1},{1,2},{2,3},{4,5},{5,6},{6,7}} | collective-permute-start | bytes 98312 | tf_op jit(solution)/shard_map/while/body/eval_jaxpr/ppermute | solution.py:89
  2866.2 8.1 copy-start.6
  2931.5 8.1 copy-start.6
  2996.8 8.1 copy-start.6
  3062.1 8.1 copy-start.6
  3127.4 8.1 copy-start.6
  3258.0 8.1 copy-start.6
  3323.3 8.1 copy-start.6
  (113 other events, 783.1 us)
where the time goes:
time: 3740 us; the launch traced here: 3730 us
  waiting for transfers between devices  2520 us (67%)
  matrix products  670 us (18%)
  local copies, waits for them, and re-layouts  219 us (6%)
  blocking collectives  157 us (4%)
  other arithmetic  108 us (3%)
    ppermute x12, waiting for transfers between devices, chain_turn(): lax.ppermute(state_piece, 'seq', shift_pairs)  2520 us
    psum x1, blocking collectives, local_fn(): return lax.psum(part_out, 'heads').astype(jnp.bfloat16)  157 us
    dot_general x12, matrix products, inner_step(): g_w_two = jnp.einsum('mgf,mgd->gfd', hidden, d_two, precision=FULL_PREC)  118 us
    dot_general x12, matrix products, inner_step(): g_w_one = jnp.einsum('mgd,mgf->gdf', key_blk, d_one, precision=FULL_PREC)  113 us
    dot_general x12, matrix products, inner_apply(): jnp.einsum('mgf,gfd->mgd', hidden, w_two, precision=FULL_PREC) + b_two  95 us
    dot_general x12, matrix products, inner_step(): jnp.einsum('mgf,gfd->mgd', hidden, w_two, precision=FULL_PREC) + b_two  90.8 us
    dot_general x12, matrix products, inner_step(): jnp.einsum('mgd,gdf->mgf', key_blk, w_one, precision=FULL_PREC) + b_one  87.8 us
  transfers between devices with their start and end apart: 12, of which 3 were waited for; matrix products, arithmetic and copies ran while one was open for 1% of the time, Pallas kernels for 0%

commit v1 on v0

v1 whole, which is shorter than its diff:
```python
import functools

import jax
import jax.numpy as jnp
from jax import lax
from jax.experimental import pallas as pl
from jax.experimental.pallas import tpu as pltpu
from jax.sharding import PartitionSpec as P

MINI_BATCH = 16
LN_EPS = 1e-6
GELU_C0 = 0.7978845608028654
GELU_C1 = 0.044715
f32 = jnp.float32
bf16 = jnp.bfloat16


def split3(val):
    high = val.astype(bf16)
    rest = val - high.astype(f32)
    mid = rest.astype(bf16)
    return high, mid, (rest - mid.astype(f32)).astype(bf16)


def dot_nn(lhs, rhs):
    return lax.dot_general(lhs, rhs, (((1,), (0,)), ((), ())), preferred_element_type=f32)


def dot_nt(lhs, rhs):
    return lax.dot_general(lhs, rhs, (((1,), (1,)), ((), ())), preferred_element_type=f32)


def dot_tn(lhs, rhs):
    return lax.dot_general(lhs, rhs, (((0,), (0,)), ((), ())), preferred_element_type=f32)


def rows(*parts):
    return jnp.concatenate(parts, 0)


def lanes(*parts):
    return jnp.concatenate(parts, 1)


def rep8(val, count):
    return rows(*([val] * (count // 8)))


def sum3(val, count):
    return val[0:count] + val[count:2 * count] + val[2 * count:3 * count]


def gelu_and_slope(z_val, key_rows):
    square = z_val * z_val
    tanh_val = jnp.tanh(z_val * (GELU_C0 + (GELU_C0 * GELU_C1) * square))
    half = 0.5 * z_val
    act = half + half * tanh_val
    tanh_key = tanh_val[:key_rows]
    slope = (0.5 + 0.5 * tanh_key) + half[:key_rows] * (1.0 - tanh_key * tanh_key) * (GELU_C0 + (3 * GELU_C0 * GELU_C1) * square[:key_rows])
    return act, slope


def inner_kernel(steps, groups, heads, k_ref, q_ref, v_ref, w1_in, w2_in, b1_in, b2_in, gain, bias, rate, o_ref,
                 w1, w2, w1_parts, w2_parts, b1, b2, act, slope, d_two, d_one, key_t, key_dup, query_dup, value_dup):
    low = lax.broadcasted_iota(jnp.int32, (16, 128), 1) < 64
    pad64 = jnp.zeros((64, 256), bf16)
    one = jnp.ones((16, 128), bf16)
    zero = jnp.zeros((16, 128), bf16)

    @pl.loop(0, groups)
    def _(g):
        for h in range(heads):
            first, second = w1_in[h], w2_in[h]
            w1[g, h] = first
            w2[g, h] = second
            w1_parts[g, h] = rows(*split3(first))
            w2_parts[g, h] = rows(*split3(second))
            b1[g, h] = b1_in[h]
            b2[g, h] = b2_in[h]

    def both_halves(tile):
        turned = pltpu.roll(tile, 64, 1)
        return jnp.where(low, tile, turned), jnp.where(low, turned, tile)

    def stage_hidden(g, k_step, q_step):
        for pair in range(heads // 2):
            cols = slice(128 * pair, 128 * pair + 128)
            keys = both_halves(k_ref[g, k_step, :, cols])
            queries = both_halves(q_ref[g, q_step, :, cols])
            values = both_halves(v_ref[g, k_step, :, cols])
            for side in range(2):
                h = 2 * pair + side
                key_dup[g, h] = keys[side]
                query_dup[g, h] = queries[side]
                value_dup[g, h] = values[side]
                kp = split3(keys[side])
                qp = split3(queries[side])
                key_t[g, h] = rows(jnp.where(low, kp[0], one), jnp.where(low, kp[1], zero), jnp.where(low, kp[2], zero))
                lhs = rows(kp[0], qp[0], kp[1], qp[1], kp[2], qp[2])
                z_one = sum3(dot_nn(lanes(lhs, lhs), rows(w1_parts[g, h], pad64)), 32) + rep8(b1[g, h], 32)
                hidden, slope_val = gelu_and_slope(z_one, 16)
                slope[g, h] = slope_val
                act[g, h] = rows(*split3(hidden))

    def stage_norm(g, q_step):
        outs = []
        for h in range(heads):
            raw = sum3(dot_nt(act[g, h], rows(w2_parts[g, h], pad64)), 32)
            folded = raw[:, :128] + raw[:, 128:]
            z_two = folded + pltpu.roll(folded, 64, 1) + rep8(b2[g, h], 32)
            centered = z_two - jnp.sum(z_two, 1, keepdims=True) * (1 / 128)
            inv_std = lax.rsqrt(jnp.sum(centered * centered, 1, keepdims=True) * (1 / 128) + LN_EPS)
            normed = centered * inv_std
            gain_h = gain[h]
            out = rows(key_dup[g, h], query_dup[g, h]) + (normed * rep8(gain_h, 32) + rep8(bias[h], 32))
            outs.append(out[16:])
            d_norm = (2.0 * (out[:16] - value_dup[g, h])) * rep8(gain_h, 16)
            normed_k = normed[:16]
            mean_d = jnp.sum(d_norm, 1, keepdims=True) * (1 / 128)
            mean_dn = jnp.sum(d_norm * normed_k, 1, keepdims=True) * (1 / 128)
            d_val = inv_std[:16] * (d_norm - mean_d - normed_k * mean_dn)
            d_two[g, h] = rows(*split3(d_val))
            total = d_val[:8] + d_val[8:]
            for shift in (4, 2, 1):
                total = total + pltpu.roll(total, shift, 0)
            b2[g, h] = b2[g, h] - rate[h] * total
        for pair in range(heads // 2):
            o_ref[g, q_step, :, 128 * pair:128 * pair + 128] = jnp.where(low, outs[2 * pair], outs[2 * pair + 1]).astype(bf16)

    def stage_second(g):
        for h in range(heads):
            dp = d_two[g, h]
            d_hidden = sum3(dot_nn(lanes(dp, dp), rows(w2_parts[g, h], pad64)), 16)
            d_one[g, h] = rows(*split3(d_hidden * slope[g, h]))
            lhs = rows(dp[:16], dp[:16], dp[:16], dp[16:32], dp[16:32], dp[32:])[:, :64]
            acts = act[g, h]
            high, mid, low_part = acts[0:16], acts[32:48], acts[64:80]
            grad = dot_tn(lhs, rows(high, mid, low_part, high, mid, high))
            new = w2[g, h] - rate[h] * grad
            w2[g, h] = new
            w2_parts[g, h] = rows(*split3(new))

    def stage_first(g):
        for h in range(heads):
            kt = key_t[g, h]
            dp = d_one[g, h]
            lhs = rows(kt[:16], kt[:16], kt[:16], kt[16:32], kt[16:32], kt[32:])[:, :80]
            grad = dot_tn(lhs, rows(dp, dp[0:32], dp[0:16]))
            new = w1[g, h] - rate[h] * grad[:64]
            w1[g, h] = new
            w1_parts[g, h] = rows(*split3(new))
            b1[g, h] = b1[g, h] - rate[h] * grad[64:72]

    def body(step, first=False, last=False):
        for turn in range(groups):
            for stage in range(4):
                before = turn < stage
                g = (turn - stage) % groups
                if (first and before) or (last and not before and stage >= 2):
                    continue
                at = step - 1 if before else step
                q_step = jnp.maximum(at - 1, 0)
                if stage == 0:
                    stage_hidden(g, jnp.minimum(at, steps - 1), q_step)
                elif stage == 1:
                    stage_norm(g, q_step)
                elif stage == 2:
                    stage_second(g)
                else:
                    stage_first(g)

    body(jnp.int32(0), first=True)

    def loop_body(step, carry):
        body(step)
        return carry

    lax.fori_loop(1, steps, loop_body, 0)
    body(jnp.int32(steps), last=True)
    stage_norm(groups - 1, steps - 1)


def run_inner(keys, queries, values, w1, w2t, b1, b2, gain, bias, rate):
    groups, steps = keys.shape[:2]
    heads = w1.shape[0]
    vmem = pl.BlockSpec(memory_space=pltpu.VMEM)
    smem = pl.BlockSpec(memory_space=pltpu.SMEM)
    per_pair = (groups, heads)
    scratch = [((64, 256), f32), ((64, 256), f32), ((192, 256), bf16), ((192, 256), bf16), ((8, 256), f32), ((8, 128), f32),
               ((96, 256), bf16), ((16, 256), f32), ((48, 128), bf16), ((48, 256), bf16), ((48, 128), bf16),
               ((16, 128), f32), ((16, 128), f32), ((16, 128), f32)]
    return pl.pallas_call(
        functools.partial(inner_kernel, steps, groups, heads),
        out_shape=jax.ShapeDtypeStruct(keys.shape, bf16),
        in_specs=[vmem] * 9 + [smem],
        out_specs=vmem,
        scratch_shapes=[pltpu.VMEM(per_pair + shape, dtype) for shape, dtype in scratch],
        compiler_params=pltpu.CompilerParams(vmem_limit_bytes=60 * 2 ** 20),
    )(keys, queries, values, w1, w2t, b1, b2, gain, bias, rate)


def solution(mesh):
    def local_fn(tokens, theta_q, theta_k, theta_v, w_out, w_one, b_one, w_two, b_two, ln_gain, ln_bias, inner_lr):
        tok_local, model_dim = tokens.shape[1:]
        heads = w_one.shape[0]
        seqs = lax.all_to_all(tokens, 'seq', 0, 1, tiled=True)
        num_seqs, seq_len = seqs.shape[:2]
        steps = seq_len // MINI_BATCH

        def project(weight):
            out = jnp.dot(seqs.reshape(num_seqs * seq_len, model_dim), weight, preferred_element_type=f32)
            return out.reshape(num_seqs, steps, MINI_BATCH, weight.shape[1])

        def eight(vec, twice):
            vec = jnp.concatenate([vec, vec], -1) if twice else vec
            return jnp.broadcast_to(vec[:, None, :], (heads, 8, vec.shape[-1]))

        outs = run_inner(project(theta_k), project(theta_q), project(theta_v), w_one, jnp.swapaxes(w_two, 1, 2), eight(b_one, False),
                         eight(b_two, True), eight(ln_gain, True), eight(ln_bias, True), inner_lr / MINI_BATCH)
        outs = outs.reshape(num_seqs, seq_len, outs.shape[-1])
        outs = lax.all_to_all(outs, 'seq', 1, 0, tiled=True)
        outs = lax.all_gather(outs, 'heads', axis=2, tiled=True)
        w_full = lax.all_gather(w_out, 'heads', axis=0, tiled=True)
        return jnp.einsum('bte,ed->btd', outs, w_full, preferred_element_type=f32).astype(bf16)

    arg_specs = (P('data', 'seq', None), P(None, 'heads'), P(None, 'heads'), P(None, 'heads'), P('heads', None), P('heads', None, None), P('heads', None), P('heads', None, None), P('heads', None), P('heads', None), P('heads', None), P('heads'))
    return jax.shard_map(local_fn, mesh=mesh, in_specs=arg_specs, out_specs=P('data', 'seq', None), check_vma=False)
```

time: 3740 us -> 458 us (0.12)
  waiting for transfers between devices: 2520 us -> 182 us
  matrix products: 670 us -> 27.2 us
  Pallas kernels: 0 us -> 206 us
  local copies, waits for them, and re-layouts: 219 us -> 14.3 us
  blocking collectives: 157 us -> 0 us
  other arithmetic: 108 us -> 0.81 us
    ppermute x12 -> x0, waiting for transfers between devices: 2520 us -> none  [chain_turn(): lax.ppermute(state_piece, 'seq', shift_pairs)]
    dot_general x88 -> x4, matrix products: 670 us -> 27.2 us  [the longest x3 16.1 us: project(): jnp.dot(seqs.reshape(num_seqs * seq_len, model_dim), weight, preferred_el...]
    pallas_call x0 -> x1, Pallas kernels: none -> 206 us  [run_inner(): pl.pallas_call(functools.partial(inner_kernel, steps, groups, heads), out...]
    psum x1 -> x0, blocking collectives: 157 us -> none  [local_fn(): return lax.psum(part_out, 'heads').astype(jnp.bfloat16)]
    all_to_all x0 -> x2, waiting for transfers between devices: none -> 101 us  [the longest x1 67 us: local_fn(): seqs = lax.all_to_all(tokens, 'seq', 0, 1, tiled=True)]
    all_gather x0 -> x2, waiting for transfers between devices: none -> 80 us  [the longest x1 79.9 us: local_fn(): outs = lax.all_gather(outs, 'heads', axis=2, tiled=True)]
    reduce_sum x48 -> x0, other arithmetic: 77.2 us -> none  [the longest x12 41.8 us: inner_step(): jnp.mean(d_norm, axis=-1, keepdims=True)]
    unnamed x26 -> x18, local copies, waits for them, and re-layouts: 56.3 us -> 0.04 us
  transfers between devices with their start and end apart: 12 -> 4, of which waited for: 3 -> 3; matrix products, arithmetic and copies ran while one was open for 1% -> 1% of each run, Pallas kernels for 0% -> 0%
where the time goes in v1:
time: 458 us; the launch traced here: 456 us
  Pallas kernels  206 us (45%)
  waiting for transfers between devices  182 us (40%)
  matrix products  27.2 us (6%)
  local copies, waits for them, and re-layouts  14.3 us (3%)
  between operations  13.5 us (3%)
  starting transfers between devices  11.6 us (3%)
    pallas_call x1, Pallas kernels, run_inner(): pl.pallas_call(functools.partial(inner_kernel, steps, groups, heads), out...  206 us
    all_gather x1, waiting for transfers between devices, local_fn(): outs = lax.all_gather(outs, 'heads', axis=2, tiled=True)  79.9 us
    all_to_all x1, waiting for transfers between devices, local_fn(): seqs = lax.all_to_all(tokens, 'seq', 0, 1, tiled=True)  67 us
    all_to_all x1, waiting for transfers between devices, local_fn(): outs = lax.all_to_all(outs, 'seq', 1, 0, tiled=True)  34.1 us
    dot_general x3, matrix products, project(): jnp.dot(seqs.reshape(num_seqs * seq_len, model_dim), weight, preferred_el...  16.1 us
    dot_general x1, matrix products, local_fn(): jnp.einsum('bte,ed->btd', outs, w_full, preferred_element_type=f32)  11.2 us
  transfers between devices with their start and end apart: 4, of which 3 were waited for; matrix products, arithmetic and copies ran while one was open for 1% of the time, Pallas kernels for 0%

profile of v1, /device:TPU:3, one launch (start us, length us, event | category | flops | bytes accessed | tf_op | source)
XLA Modules:
  0.0 455.6 jit_solution(18293179093118530023)
XLA Ops:
  6.5 5.4 %all-to-all-start = ((bf16[16,192,1024]{2,1,0:T(8,128)(2,1)}), bf16[16,192,1024]{2,1,0:T(8,128)(2,1)}, u32[]{:S(2)}, u32[]{:S(2)}) async-start(bf16[16,192,1024]{2,1,0:T(8,128)(2,1)} %param.12), calls=%async_computation | async-start | bytes 12582912 | tf_op jit(solution)/shard_map/all_to_all | solution.py:206
  12.0 0.1 pad_maximum_fusion.1
  12.1 0.1 pad_maximum_fusion.2
  12.1 0.1 pad_maximum_fusion
  12.2 0.6 broadcast_multiply_fusion.rate
  12.8 67.0 %all-to-all-done = bf16[16,192,1024]{2,1,0:T(8,128)(2,1)} async-done(((bf16[16,192,1024]{2,1,0:T(8,128)(2,1)}), bf16[16,192,1024]{2,1,0:T(8,128)(2,1)}, u32[]{:S(2)}, u32[]{:S(2)}) %all-to-all-start) | async-done | bytes 6291488 | tf_op jit(solution)/shard_map/all_to_all | solution.py:206
  79.8 3.5 copy.15
  83.4 5.3 %fusion.1.v_ref = f32[4,48,16,512]{3,2,1,0:T(8,128)} fusion(bf16[4,48,16,1024]{3,2,1,0:T(8,128)(2,1)S(1)} %bitcast.35, bf16[1024,512]{1,0:T(8,128)(2,1)S(1)} %copy-done), kind=kOutput, calls=%fused_computation.2 | convolution fusion | flops 3221225472 | bytes 13631488 | tf_op jit(solution)/shard_map/dot_general | solution.py:211
  88.7 5.4 %fusion.3.q_ref = f32[4,48,16,512]{3,2,1,0:T(8,128)} fusion(bf16[4,48,16,1024]{3,2,1,0:T(8,128)(2,1)S(1)} %bitcast.36, bf16[1024,512]{1,0:T(8,128)(2,1)S(1)} %copy-done.6), kind=kOutput, calls=%fused_computation.4 | convolution fusion | flops 3221225472 | bytes 13631488 | tf_op jit(solution)/shard_map/dot_general | solution.py:211
  94.1 5.4 %fusion.5.k_ref = f32[4,48,16,512]{3,2,1,0:T(8,128)} fusion(bf16[4,48,16,1024]{3,2,1,0:T(8,128)(2,1)S(1)} %bitcast.37, bf16[1024,512]{1,0:T(8,128)(2,1)S(1)} %copy-done.7), kind=kOutput, calls=%fused_computation.6 | convolution fusion | flops 3221225472 | bytes 13631488 | tf_op jit(solution)/shard_map/dot_general | solution.py:211
  99.4 0.6 broadcast_in_dim.8.b1_in
  100.1 0.6 broadcast_in_dim.10.gain
  100.7 0.6 broadcast_in_dim.11.bias
  101.3 0.6 broadcast_in_dim.9.b2_in
  101.9 206.3 %shard_map.118 = bf16[4,48,16,512]{3,2,1,0:T(8,128)(2,1)} custom-call(f32[4,48,16,512]{3,2,1,0:T(8,128)} %fusion.5.k_ref, f32[4,48,16,512]{3,2,1,0:T(8,128)} %fusion.3.q_ref, f32[4,48,16,512]{3,2,1,0:T(8,128)} %fusion.1.v_ref, f32[8,64,256]{2,1,0:T(8,128)} %w1_in.1, f32[8,64,256]{2,1,0:T(8,128)} %bitcast.38, f32[8,8,256]{2,1,0:T(8,128)} %broadcast_in_dim.8.b1_in, ...), custom_call_target="tpu_custom_call" | custom-call | tf_op jit(solution)/shard_map/pallas_call | solution.py:192
  308.2 6.0 %copy.16 = bf16[4,768,512]{2,0,1:T(4,128)(2,1)} copy(bf16[4,768,512]{2,1,0:T(8,128)(2,1)} %bitcast.32) | data formatting | bytes 6291456 | tf_op jit(solution)/shard_map/reshape | solution.py:220
  314.2 6.2 %all-to-all-start.1 = ((bf16[4,768,512]{2,0,1:T(4,128)(2,1)}), bf16[4,768,512]{2,0,1:T(4,128)(2,1)S(1)}, u32[]{:S(2)}, u32[]{:S(2)}) async-start(bf16[4,768,512]{2,0,1:T(4,128)(2,1)} %copy.16), calls=%async_computation.1 | async-start | bytes 6291456 | tf_op jit(solution)/shard_map/all_to_all | solution.py:221
  320.4 0.7 all-gather.5.cloned.1.call-update
  321.1 0.0 all-gather.3.cloned.1.call-start
  321.1 34.1 %all-to-all-done.1 = bf16[4,768,512]{2,0,1:T(4,128)(2,1)S(1)} async-done(((bf16[4,768,512]{2,0,1:T(4,128)(2,1)}), bf16[4,768,512]{2,0,1:T(4,128)(2,1)S(1)}, u32[]{:S(2)}, u32[]{:S(2)}) %all-to-all-start.1) | async-done | bytes 3145760 | tf_op jit(solution)/shard_map/all_to_all | solution.py:221
  355.2 2.4 copy.17
  357.6 0.0 all-gather.5.cloned.1.call-done
  357.7 79.9 %all-gather.3.cloned.1.call-done = bf16[16,192,1024]{2,1,0:T(8,128)(2,1)} async-done(((bf16[16,192,512]{2,1,0:T(8,128)(2,1)}), bf16[16,192,1024]{2,1,0:T(8,128)(2,1)}) %all-gather.3.cloned.1.call-update) | async-done | bytes 6291472 | tf_op jit(solution)/shard_map/all_gather | solution.py:222
  437.6 11.2 %convolution_convert_fusion = bf16[16,192,1024]{2,1,0:T(8,128)(2,1)} fusion(bf16[16,192,1024]{2,1,0:T(8,128)(2,1)} %all-gather.3.cloned.1.call-done, bf16[1024,1024]{1,0:T(8,128)(2,1)} %all-gather.5.cloned.1.call-done), kind=kOutput, calls=%fused_computation | convolution fusion | flops 6445596672 | bytes 14680064 | tf_op jit(solution)/shard_map/bte,ed->btd/dot_general | solution.py:224
  (20 shorter events, 0.1 us)
Async XLA Ops:
  6.5 76.8 %copy-start = (bf16[1024,512]{1,0:T(8,128)(2,1)S(1)}, bf16[1024,512]{1,0:T(8,128)(2,1)}, u32[]{:S(2)}) copy-start(bf16[1024,512]{1,0:T(8,128)(2,1)} %param.15) | copy-start | bytes 3145732
  6.5 5.4 %copy-start.3 = (f32[8,64]{1,0:T(8,128)S(1)}, f32[8,64]{1,0:T(8,128)}, u32[]{:S(2)}) copy-start(f32[8,64]{1,0:T(8,128)} %param.21) | copy-start | bytes 6148
  6.5 5.5 %copy-start.4 = (f32[8,64]{1,0:T(8,128)S(1)}, f32[8,64]{1,0:T(8,128)}, u32[]{:S(2)}) copy-start(f32[8,64]{1,0:T(8,128)} %param.22) | copy-start | bytes 6148
  6.5 5.6 %copy-start.5 = (f32[8,64]{1,0:T(8,128)S(1)}, f32[8,64]{1,0:T(8,128)}, u32[]{:S(2)}) copy-start(f32[8,64]{1,0:T(8,128)} %param.20) | copy-start | bytes 6148
  6.5 5.7 %copy-start.8 = (f32[8]{0:T(128)S(1)}, f32[8]{0:T(128)}, u32[]{:S(2)}) copy-start(f32[8]{0:T(128)} %param.23) | copy-start | bytes 100
  6.5 73.3 %all-to-all-start = ((bf16[16,192,1024]{2,1,0:T(8,128)(2,1)}), bf16[16,192,1024]{2,1,0:T(8,128)(2,1)}, u32[]{:S(2)}, u32[]{:S(2)}) async-start(bf16[16,192,1024]{2,1,0:T(8,128)(2,1)} %param.12), calls=%async_computation | async-start | bytes 12582912 | tf_op jit(solution)/shard_map/all_to_all | solution.py:206
  83.4 5.4 %copy-start.6 = (bf16[1024,512]{1,0:T(8,128)(2,1)S(1)}, bf16[1024,512]{1,0:T(8,128)(2,1)}, u32[]{:S(2)}) copy-start(bf16[1024,512]{1,0:T(8,128)(2,1)} %param.13) | copy-start | bytes 3145732
  88.7 5.4 %copy-start.7 = (bf16[1024,512]{1,0:T(8,128)(2,1)S(1)}, bf16[1024,512]{1,0:T(8,128)(2,1)}, u32[]{:S(2)}) copy-start(bf16[1024,512]{1,0:T(8,128)(2,1)} %param.14) | copy-start | bytes 3145732
  94.1 5.4 %copy-start.2 = (f32[8,256]{1,0:T(8,128)S(1)}, f32[8,256]{1,0:T(8,128)}, u32[]{:S(2)}) copy-start(f32[8,256]{1,0:T(8,128)} %param.18) | copy-start | bytes 24580
  314.2 41.0 %all-to-all-start.1 = ((bf16[4,768,512]{2,0,1:T(4,128)(2,1)}), bf16[4,768,512]{2,0,1:T(4,128)(2,1)S(1)}, u32[]{:S(2)}, u32[]{:S(2)}) async-start(bf16[4,768,512]{2,0,1:T(4,128)(2,1)} %copy.16), calls=%async_computation.1 | async-start | bytes 6291456 | tf_op jit(solution)/shard_map/all_to_all | solution.py:221
  320.4 37.3 %all-gather.5.cloned.1.call-start = ((), (), s32[]{:S(2)}) async-start(), calls=%async_computation.3 | async-start | bytes 3145728 | tf_op jit(solution)/shard_map/all_gather | solution.py:223
  321.1 116.5 %all-gather.3.cloned.1.call-start = ((), (), s32[]{:S(2)}) async-start(), calls=%async_computation.2 | async-start | bytes 9437184 | tf_op jit(solution)/shard_map/all_gather | solution.py:222
  437.6 11.2 %copy-start.1 = (bf16[1024,512]{1,0:T(8,128)(2,1)S(1)}, bf16[1024,512]{1,0:T(8,128)(2,1)}, u32[]{:S(2)}) copy-start(bf16[1024,512]{1,0:T(8,128)(2,1)} %param.15) | copy-start | bytes 3145732
Sparse Core Ops, SparseCore 0:
  322.7 31.3 all-gather.4
  357.7 79.7 all-gather.2

commit v2 on v1

--- a/solution.py
+++ b/solution.py
@@ -60,8 +60,14 @@
     return act, slope
 
 
-def inner_kernel(steps, groups, heads, k_ref, q_ref, v_ref, w1_in, w2_in, b1_in, b2_in, gain, bias, rate, o_ref,
-                 w1, w2, w1_parts, w2_parts, b1, b2, act, slope, d_two, d_one, key_t, key_dup, query_dup, value_dup):
+def inner_kernel(steps, groups, heads, k_ref, q_ref, v_ref, w1_in, w2_in, b1_in, b2_in, gain, bias, rate, w_mine, o_ref, w_other,
+                 w1, w2, w1_parts, w2_parts, b1, b2, act, slope, d_two, d_one, key_t, key_dup, query_dup, value_dup, send_sem, recv_sem):
+    peer = {'heads': 1 - lax.axis_index('heads')}
+    barrier = pltpu.get_barrier_semaphore()
+    pl.semaphore_signal(barrier, inc=1, device_id=peer, device_id_type=pl.DeviceIdType.MESH)
+    pl.semaphore_wait(barrier, 1)
+    swap = pltpu.make_async_remote_copy(w_mine, w_other, send_sem, recv_sem, device_id=peer, device_id_type=pl.DeviceIdType.MESH)
+    swap.start()
     low = lax.broadcasted_iota(jnp.int32, (16, 128), 1) < 64
     pad64 = jnp.zeros((64, 256), bf16)
     one = jnp.ones((16, 128), bf16)
@@ -178,12 +184,14 @@
     lax.fori_loop(1, steps, loop_body, 0)
     body(jnp.int32(steps), last=True)
     stage_norm(groups - 1, steps - 1)
-
-
-def run_inner(keys, queries, values, w1, w2t, b1, b2, gain, bias, rate):
+    swap.wait()
+
+
+def run_inner(keys, queries, values, w1, w2t, b1, b2, gain, bias, rate, w_out):
     groups, steps = keys.shape[:2]
     heads = w1.shape[0]
     vmem = pl.BlockSpec(memory_space=pltpu.VMEM)
+    hbm = pl.BlockSpec(memory_space=pl.ANY)
     smem = pl.BlockSpec(memory_space=pltpu.SMEM)
     per_pair = (groups, heads)
     scratch = [((64, 256), f32), ((64, 256), f32), ((192, 256), bf16), ((192, 256), bf16), ((8, 256), f32), ((8, 128), f32),
@@ -191,12 +199,12 @@
                ((16, 128), f32), ((16, 128), f32), ((16, 128), f32)]
     return pl.pallas_call(
         functools.partial(inner_kernel, steps, groups, heads),
-        out_shape=jax.ShapeDtypeStruct(keys.shape, bf16),
-        in_specs=[vmem] * 9 + [smem],
-        out_specs=vmem,
-        scratch_shapes=[pltpu.VMEM(per_pair + shape, dtype) for shape, dtype in scratch],
-        compiler_params=pltpu.CompilerParams(vmem_limit_bytes=60 * 2 ** 20),
-    )(keys, queries, values, w1, w2t, b1, b2, gain, bias, rate)
+        out_shape=(jax.ShapeDtypeStruct(keys.shape, bf16), jax.ShapeDtypeStruct(w_out.shape, bf16)),
+        in_specs=[vmem] * 9 + [smem, hbm],
+        out_specs=(vmem, hbm),
+        scratch_shapes=[pltpu.VMEM(per_pair + shape, dtype) for shape, dtype in scratch] + [pltpu.SemaphoreType.DMA] * 2,
+        compiler_params=pltpu.CompilerParams(vmem_limit_bytes=60 * 2 ** 20, collective_id=0, has_side_effects=True),
+    )(keys, queries, values, w1, w2t, b1, b2, gain, bias, rate, w_out)
 
 
 def solution(mesh):
@@ -215,12 +223,13 @@
             vec = jnp.concatenate([vec, vec], -1) if twice else vec
             return jnp.broadcast_to(vec[:, None, :], (heads, 8, vec.shape[-1]))
 
-        outs = run_inner(project(theta_k), project(theta_q), project(theta_v), w_one, jnp.swapaxes(w_two, 1, 2), eight(b_one, False),
-                         eight(b_two, True), eight(ln_gain, True), eight(ln_bias, True), inner_lr / MINI_BATCH)
+        outs, w_other = run_inner(project(theta_k), project(theta_q), project(theta_v), w_one, jnp.swapaxes(w_two, 1, 2), eight(b_one, False),
+                         eight(b_two, True), eight(ln_gain, True), eight(ln_bias, True), inner_lr / MINI_BATCH, w_out)
         outs = outs.reshape(num_seqs, seq_len, outs.shape[-1])
         outs = lax.all_to_all(outs, 'seq', 1, 0, tiled=True)
         outs = lax.all_gather(outs, 'heads', axis=2, tiled=True)
-        w_full = lax.all_gather(w_out, 'heads', axis=0, tiled=True)
+        first = lax.axis_index('heads') == 0
+        w_full = jnp.concatenate([jnp.where(first, w_out, w_other), jnp.where(first, w_other, w_out)], 0)
         return jnp.einsum('bte,ed->btd', outs, w_full, preferred_element_type=f32).astype(bf16)
 
     arg_specs = (P('data', 'seq', None), P(None, 'heads'), P(None, 'heads'), P(None, 'heads'), P('heads', None), P('heads', None, None), P('heads', None), P('heads', None, None), P('heads', None), P('heads', None), P('heads', None), P('heads'))

time: 458 us -> 455 us (level)
  blocking collectives: 0 us -> 39.6 us
  waiting for transfers between devices: 182 us -> 144 us
  starting transfers between devices: 11.6 us -> 5.45 us
    all_to_all x0 -> x1, blocking collectives: none -> 39.6 us  [local_fn(): outs = lax.all_to_all(outs, 'seq', 1, 0, tiled=True)]
    all_to_all x1 -> x0, waiting for transfers between devices: 34.1 us -> none  [local_fn(): outs = lax.all_to_all(outs, 'seq', 1, 0, tiled=True)]
    all_to_all x1 -> x0, starting transfers between devices: 6.18 us -> none  [local_fn(): outs = lax.all_to_all(outs, 'seq', 1, 0, tiled=True)]
  transfers between devices with their start and end apart: 4 -> 2, of which waited for: 3 -> 2; matrix products, arithmetic and copies ran while one was open for 1% -> 0% of each run, Pallas kernels for 0% -> 0%
where the time goes in v2:
time: 455 us; the launch traced here: 453 us
  Pallas kernels  209 us (46%)
  waiting for transfers between devices  144 us (32%)
  blocking collectives  39.6 us (9%)
  matrix products  26.9 us (6%)
  between operations  13.5 us (3%)
  local copies, waits for them, and re-layouts  12.7 us (3%)
  starting transfers between devices  5.45 us (1%)
    pallas_call x1, Pallas kernels, run_inner(): pl.pallas_call(functools.partial(inner_kernel, steps, groups, heads), out...  209 us
    all_gather x1, waiting for transfers between devices, local_fn(): outs = lax.all_gather(outs, 'heads', axis=2, tiled=True)  76.9 us
    all_to_all x1, waiting for transfers between devices, local_fn(): seqs = lax.all_to_all(tokens, 'seq', 0, 1, tiled=True)  67 us
    all_to_all x1, blocking collectives, local_fn(): outs = lax.all_to_all(outs, 'seq', 1, 0, tiled=True)  39.6 us
    dot_general x3, matrix products, project(): jnp.dot(seqs.reshape(num_seqs * seq_len, model_dim), weight, preferred_el...  16.1 us
    dot_general x1, matrix products, local_fn(): jnp.einsum('bte,ed->btd', outs, w_full, preferred_element_type=f32)  10.8 us
  transfers between devices with their start and end apart: 2, of which 2 were waited for; matrix products, arithmetic and copies ran while one was open for 0% of the time, Pallas kernels for 0%

profile of v2, /device:TPU:3, one launch (start us, length us, event | category | flops | bytes accessed | tf_op | source)
XLA Modules:
  0.0 453.1 jit_solution(3358199543298989989)
XLA Ops:
  6.5 5.4 %all-to-all-start = ((bf16[16,192,1024]{2,1,0:T(8,128)(2,1)}), bf16[16,192,1024]{2,1,0:T(8,128)(2,1)}, u32[]{:S(2)}, u32[]{:S(2)}) async-start(bf16[16,192,1024]{2,1,0:T(8,128)(2,1)} %param.12), calls=%async_computation | async-start | bytes 12582912 | tf_op jit(solution)/shard_map/all_to_all | solution.py:214
  12.0 0.0 all-gather.2.cloned.1.call-start
  12.0 0.1 pad_maximum_fusion.1
  12.1 0.1 pad_maximum_fusion.2
  12.2 0.1 pad_maximum_fusion
  12.3 0.6 broadcast_multiply_fusion.rate
  12.9 67.0 %all-to-all-done = bf16[16,192,1024]{2,1,0:T(8,128)(2,1)} async-done(((bf16[16,192,1024]{2,1,0:T(8,128)(2,1)}), bf16[16,192,1024]{2,1,0:T(8,128)(2,1)}, u32[]{:S(2)}, u32[]{:S(2)}) %all-to-all-start) | async-done | bytes 6291488 | tf_op jit(solution)/shard_map/all_to_all | solution.py:214
  79.8 3.5 copy.15
  83.3 0.0 copy-start.8
  83.4 5.4 %fusion.2.v_ref = f32[4,48,16,512]{3,2,1,0:T(8,128)} fusion(bf16[4,48,16,1024]{3,2,1,0:T(8,128)(2,1)S(1)} %bitcast.34, bf16[1024,512]{1,0:T(8,128)(2,1)S(1)} %copy-done), kind=kOutput, calls=%fused_computation.4 | convolution fusion | flops 3221225472 | bytes 13631488 | tf_op jit(solution)/shard_map/dot_general | solution.py:219
  88.8 5.4 %fusion.4.q_ref = f32[4,48,16,512]{3,2,1,0:T(8,128)} fusion(bf16[4,48,16,1024]{3,2,1,0:T(8,128)(2,1)S(1)} %bitcast.35, bf16[1024,512]{1,0:T(8,128)(2,1)S(1)} %copy-done.8), kind=kOutput, calls=%fused_computation.6 | convolution fusion | flops 3221225472 | bytes 13631488 | tf_op jit(solution)/shard_map/dot_general | solution.py:219
  94.1 5.3 %fusion.6.k_ref = f32[4,48,16,512]{3,2,1,0:T(8,128)} fusion(bf16[4,48,16,1024]{3,2,1,0:T(8,128)(2,1)S(1)} %bitcast.36, bf16[1024,512]{1,0:T(8,128)(2,1)S(1)} %copy-done.9), kind=kOutput, calls=%fused_computation.8 | convolution fusion | flops 3221225472 | bytes 13631488 | tf_op jit(solution)/shard_map/dot_general | solution.py:219
  99.5 0.6 broadcast_in_dim.8.b1_in
  100.1 0.6 broadcast_in_dim.10.gain
  100.7 0.6 broadcast_in_dim.11.bias
  101.3 0.6 broadcast_in_dim.9.b2_in
  101.9 209.1 %shard_map.118 = (bf16[4,48,16,512]{3,2,1,0:T(8,128)(2,1)}, bf16[512,1024]{1,0:T(8,128)(2,1)}) custom-call(f32[4,48,16,512]{3,2,1,0:T(8,128)} %fusion.6.k_ref, f32[4,48,16,512]{3,2,1,0:T(8,128)} %fusion.4.q_ref, f32[4,48,16,512]{3,2,1,0:T(8,128)} %fusion.2.v_ref, f32[8,64,256]{2,1,0:T(8,128)} %w1_in.1, f32[8,64,256]{2,1,0:T(8,128)} %bitcast.38, ...), custom_call_target="tpu_custom_call" | custom-call | tf_op jit(solution)/shard_map/pallas_call | solution.py:200
  311.1 4.3 copy.16
  315.4 39.6 %all_to_all.33 = bf16[4,768,512]{2,0,1:T(4,128)(2,1)S(1)} all-to-all(bf16[4,768,512]{2,0,1:T(4,128)(2,1)S(1)} %copy.16), channel_id=1, replica_groups=mesh['data'=1,'heads'=2,'seq'=4] {'seq'}, dimensions={1} | all-to-all | bytes 6291456 | tf_op jit(solution)/shard_map/all_to_all | solution.py:229
  355.0 2.4 copy.17
  357.3 0.0 all-gather.2.cloned.1.call-update
  357.4 1.1 broadcast_select_fusion.1
  358.5 76.9 %all-gather.2.cloned.1.call-done = bf16[16,192,1024]{2,1,0:T(8,128)(2,1)} async-done(((bf16[16,192,512]{2,1,0:T(8,128)(2,1)}), bf16[16,192,1024]{2,1,0:T(8,128)(2,1)}) %all-gather.2.cloned.1.call-update) | async-done | bytes 6291472 | tf_op jit(solution)/shard_map/all_gather | solution.py:230
  435.4 10.8 %convolution_convert_fusion = bf16[16,192,1024]{2,1,0:T(8,128)(2,1)} fusion(bf16[16,192,1024]{2,1,0:T(8,128)(2,1)} %all-gather.2.cloned.1.call-done, bf16[512,1024]{1,0:T(8,128)(2,1)} %get-tuple-element.10, bf16[512,1024]{1,0:T(8,128)(2,1)S(1)} %get-tuple-element.9), kind=kOutput, calls=%fused_computation | convolution fusion | flops 6449790976 | bytes 14680064 | tf_op jit(solution)/shard_map/bte,ed->btd/dot_general | solution.py:233
  (21 shorter events, 0.0 us)
Async XLA Ops:
  6.5 76.8 %copy-start = (bf16[1024,512]{1,0:T(8,128)(2,1)S(1)}, bf16[1024,512]{1,0:T(8,128)(2,1)}, u32[]{:S(2)}) copy-start(bf16[1024,512]{1,0:T(8,128)(2,1)} %param.15) | copy-start | bytes 3145732
  6.5 5.5 %copy-start.5 = (f32[8,64]{1,0:T(8,128)S(1)}, f32[8,64]{1,0:T(8,128)}, u32[]{:S(2)}) copy-start(f32[8,64]{1,0:T(8,128)} %param.21) | copy-start | bytes 6148
  6.5 5.6 %copy-start.6 = (f32[8,64]{1,0:T(8,128)S(1)}, f32[8,64]{1,0:T(8,128)}, u32[]{:S(2)}) copy-start(f32[8,64]{1,0:T(8,128)} %param.22) | copy-start | bytes 6148
  6.5 5.6 %copy-start.7 = (f32[8,64]{1,0:T(8,128)S(1)}, f32[8,64]{1,0:T(8,128)}, u32[]{:S(2)}) copy-start(f32[8,64]{1,0:T(8,128)} %param.20) | copy-start | bytes 6148
  6.5 5.7 %copy-start.10 = (f32[8]{0:T(128)S(1)}, f32[8]{0:T(128)}, u32[]{:S(2)}) copy-start(f32[8]{0:T(128)} %param.23) | copy-start | bytes 100
  6.5 73.3 %all-to-all-start = ((bf16[16,192,1024]{2,1,0:T(8,128)(2,1)}), bf16[16,192,1024]{2,1,0:T(8,128)(2,1)}, u32[]{:S(2)}, u32[]{:S(2)}) async-start(bf16[16,192,1024]{2,1,0:T(8,128)(2,1)} %param.12), calls=%async_computation | async-start | bytes 12582912 | tf_op jit(solution)/shard_map/all_to_all | solution.py:214
  12.0 423.4 %all-gather.2.cloned.1.call-start = ((), (), s32[]{:S(2)}) async-start(), calls=%async_computation.2 | async-start | bytes 9437184 | tf_op jit(solution)/shard_map/all_gather | solution.py:230
  83.3 5.4 %copy-start.8 = (bf16[1024,512]{1,0:T(8,128)(2,1)S(1)}, bf16[1024,512]{1,0:T(8,128)(2,1)}, u32[]{:S(2)}) copy-start(bf16[1024,512]{1,0:T(8,128)(2,1)} %param.13) | copy-start | bytes 3145732
  88.8 5.4 %copy-start.9 = (bf16[1024,512]{1,0:T(8,128)(2,1)S(1)}, bf16[1024,512]{1,0:T(8,128)(2,1)}, u32[]{:S(2)}) copy-start(bf16[1024,512]{1,0:T(8,128)(2,1)} %param.14) | copy-start | bytes 3145732
  94.1 5.3 %copy-start.4 = (f32[8,256]{1,0:T(8,128)S(1)}, f32[8,256]{1,0:T(8,128)}, u32[]{:S(2)}) copy-start(f32[8,256]{1,0:T(8,128)} %param.18) | copy-start | bytes 24580
  354.9 2.4 copy-start.2
  355.0 2.4 copy-start.3
  435.4 10.8 %copy-start.1 = (bf16[1024,512]{1,0:T(8,128)(2,1)S(1)}, bf16[1024,512]{1,0:T(8,128)(2,1)}, u32[]{:S(2)}) copy-start(bf16[1024,512]{1,0:T(8,128)(2,1)} %param.15) | copy-start | bytes 3145732
Sparse Core Ops, SparseCore 0:
  357.5 77.8 all-gather.1

commit v3 on v1

--- a/solution.py
+++ b/solution.py
@@ -60,34 +60,133 @@
     return act, slope
 
 
-def inner_kernel(steps, groups, heads, k_ref, q_ref, v_ref, w1_in, w2_in, b1_in, b2_in, gain, bias, rate, o_ref,
-                 w1, w2, w1_parts, w2_parts, b1, b2, act, slope, d_two, d_one, key_t, key_dup, query_dup, value_dup):
+def eight_rows(row, twice):
+    row = lanes(row, row) if twice else row
+    return jnp.broadcast_to(row, (8, row.shape[1]))
+
+
+def layer_kernel(steps, groups, heads, parts_of_seq, tokens, theta_k, theta_q, theta_v, w_out, w1_in, w2_in, b1_in, b2_in, gain_in, bias_in, rate_in,
+                 o_full, w_full,
+                 w1, w2, w1_parts, w2_parts, b1, b2, act, slope, d_two, d_one, key_t, key_dup, query_dup, value_dup, gain, bias,
+                 tok, outs, k_now, v_now, q_now, q_next, k_new, v_new, q_new,
+                 tok_send, tok_recv, out_send, out_recv, own_sem, w_send, w_recv, w_own):
     low = lax.broadcasted_iota(jnp.int32, (16, 128), 1) < 64
     pad64 = jnp.zeros((64, 256), bf16)
     one = jnp.ones((16, 128), bf16)
     zero = jnp.zeros((16, 128), bf16)
-
-    @pl.loop(0, groups)
-    def _(g):
-        for h in range(heads):
-            first, second = w1_in[h], w2_in[h]
-            w1[g, h] = first
-            w2[g, h] = second
-            w1_parts[g, h] = rows(*split3(first))
-            w2_parts[g, h] = rows(*split3(second))
-            b1[g, h] = b1_in[h]
-            b2[g, h] = b2_in[h]
+    width = 64 * heads
+    own_steps = steps // parts_of_seq
+    row_axis = lax.axis_index('heads')
+    me = lax.axis_index('seq')
+    other_row = 1 - row_axis
+    my_cols = pl.ds(pl.multiple_of(row_axis * width, width), width)
+    mesh_ids = pl.DeviceIdType.MESH
+
+    def other_core(place):
+        return place + 1 - 2 * lax.rem(place, 2)
+
+    near = other_core(me)
+    far_a = lax.rem(me + 2, 4)
+    far_b = other_core(far_a)
+
+    barrier = pltpu.get_barrier_semaphore()
+    for shift_row in range(2):
+        for shift in range(parts_of_seq):
+            if shift_row or shift:
+                pl.semaphore_signal(barrier, inc=1, device_id={'heads': lax.rem(row_axis + shift_row, 2), 'seq': lax.rem(me + shift, parts_of_seq)}, device_id_type=mesh_ids)
+    pl.semaphore_wait(barrier, 2 * parts_of_seq - 1)
+
+    def token_copy(slot, dest, chunk):
+        at = me * own_steps + chunk
+        return pltpu.make_async_remote_copy(tokens.at[pl.ds(groups * dest, groups), pl.ds(MINI_BATCH * chunk, MINI_BATCH)], tok.at[:, at],
+                                            tok_send.at[slot, chunk], tok_recv.at[at], device_id={'seq': dest}, device_id_type=mesh_ids)
+
+    def own_tokens(chunk):
+        at = me * own_steps + chunk
+        return pltpu.make_async_copy(tokens.at[pl.ds(groups * me, groups), pl.ds(MINI_BATCH * chunk, MINI_BATCH)], tok.at[:, at], tok_recv.at[at])
+
+    def send_far():
+        @pl.loop(0, own_steps)
+        def _(chunk):
+            token_copy(1, far_a, chunk).start()
+            token_copy(2, far_b, chunk).start()
+
+    @pl.when(lax.rem(me, 2) == 0)
+    def _():
+        send_far()
+
+    @pl.loop(0, own_steps)
+    def _(chunk):
+        own_tokens(chunk).start()
+        token_copy(0, near, chunk).start()
+
+    def wait_tokens(step):
+        pltpu.make_async_remote_copy(tokens.at[pl.ds(0, groups), pl.ds(0, MINI_BATCH)], tok.at[:, step], tok_send.at[0, 0], tok_recv.at[step],
+                                     device_id={'seq': near}, device_id_type=mesh_ids).wait_recv()
+
+    my_w_rows = w_full.at[pl.ds(pl.multiple_of(row_axis * width, width), width)]
+    w_swap = pltpu.make_async_remote_copy(w_out, my_w_rows, w_send, w_recv, device_id={'heads': other_row}, device_id_type=mesh_ids)
+    w_keep = pltpu.make_async_copy(w_out, my_w_rows, w_own)
+    w_swap.start()
+    w_keep.start()
+
+    def out_target(step, place):
+        return o_full.at[pl.ds(groups * place, groups), pl.ds(MINI_BATCH * lax.rem(step, own_steps), MINI_BATCH), my_cols]
+
+    def send_out(step):
+        owner = step // own_steps
+        across = pltpu.make_async_remote_copy(outs.at[:, step], out_target(step, me), out_send.at[1], out_recv.at[row_axis, me],
+                                              device_id={'heads': other_row, 'seq': owner}, device_id_type=mesh_ids)
+        across.start()
+
+        @pl.when(owner != me)
+        def _():
+            pltpu.make_async_remote_copy(outs.at[:, step], out_target(step, me), out_send.at[0], out_recv.at[row_axis, me],
+                                         device_id={'seq': owner}, device_id_type=mesh_ids).start()
+
+        @pl.when(owner == me)
+        def _():
+            pltpu.make_async_copy(outs.at[:, step], out_target(step, me), own_sem).start()
+
+    for h in range(heads):
+        b1[0, h] = eight_rows(b1_in[h:h + 1], False)
+        b2[0, h] = eight_rows(b2_in[h:h + 1], True)
+        gain[h] = eight_rows(gain_in[h:h + 1], True)
+        bias[h] = eight_rows(bias_in[h:h + 1], True)
+        first, second = rows(*split3(w1_in[h])), rows(*split3(w2_in[h]))
+        for g in range(groups):
+            w1[g, h] = w1_in[h]
+            w2[g, h] = w2_in[h]
+            w1_parts[g, h] = first
+            w2_parts[g, h] = second
+            if g:
+                b1[g, h] = b1[0, h]
+                b2[g, h] = b2[0, h]
+    q_next[...] = jnp.zeros(q_next.shape, f32)
+    rate = [rate_in[h] * (1 / MINI_BATCH) for h in range(heads)]
+
+    def project(step):
+        toks = tok[:, step].reshape(groups * MINI_BATCH, tok.shape[3])
+        for theta, target in ((theta_k, k_new), (theta_q, q_new), (theta_v, v_new)):
+            for col in range(0, width, 256):
+                target[:, :, col:col + 256] = dot_nn(toks, theta[:, col:col + 256]).reshape(groups, MINI_BATCH, 256)
+
+    def shift_in():
+        q_now[...] = q_next[...]
+        q_next[...] = q_new[...]
+        k_now[...] = k_new[...]
+        v_now[...] = v_new[...]
 
     def both_halves(tile):
         turned = pltpu.roll(tile, 64, 1)
         return jnp.where(low, tile, turned), jnp.where(low, turned, tile)
 
-    def stage_hidden(g, k_step, q_step):
+    def stage_hidden(g):
         for pair in range(heads // 2):
             cols = slice(128 * pair, 128 * pair + 128)
-            keys = both_halves(k_ref[g, k_step, :, cols])
-            queries = both_halves(q_ref[g, q_step, :, cols])
-            values = both_halves(v_ref[g, k_step, :, cols])
+            keys = both_halves(k_now[g, :, cols])
+            queries = both_halves(q_now[g, :, cols])
+            values = both_halves(v_now[g, :, cols])
             for side in range(2):
                 h = 2 * pair + side
                 key_dup[g, h] = keys[side]
@@ -103,7 +202,7 @@
                 act[g, h] = rows(*split3(hidden))
 
     def stage_norm(g, q_step):
-        outs = []
+        vals = []
         for h in range(heads):
             raw = sum3(dot_nt(act[g, h], rows(w2_parts[g, h], pad64)), 32)
             folded = raw[:, :128] + raw[:, 128:]
@@ -113,7 +212,7 @@
             normed = centered * inv_std
             gain_h = gain[h]
             out = rows(key_dup[g, h], query_dup[g, h]) + (normed * rep8(gain_h, 32) + rep8(bias[h], 32))
-            outs.append(out[16:])
+            vals.append(out[16:])
             d_norm = (2.0 * (out[:16] - value_dup[g, h])) * rep8(gain_h, 16)
             normed_k = normed[:16]
             mean_d = jnp.sum(d_norm, 1, keepdims=True) * (1 / 128)
@@ -125,7 +224,7 @@
                 total = total + pltpu.roll(total, shift, 0)
             b2[g, h] = b2[g, h] - rate[h] * total
         for pair in range(heads // 2):
-            o_ref[g, q_step, :, 128 * pair:128 * pair + 128] = jnp.where(low, outs[2 * pair], outs[2 * pair + 1]).astype(bf16)
+            outs[g, q_step, :, 128 * pair:128 * pair + 128] = jnp.where(low, vals[2 * pair], vals[2 * pair + 1]).astype(bf16)
 
     def stage_second(g):
         for h in range(heads):
@@ -152,6 +251,9 @@
             b1[g, h] = b1[g, h] - rate[h] * grad[64:72]
 
     def body(step, first=False, last=False):
+        shift_in()
+        if not last:
+            project(jnp.minimum(step + 1, steps - 1))
         for turn in range(groups):
             for stage in range(4):
                 before = turn < stage
@@ -159,68 +261,111 @@
                 if (first and before) or (last and not before and stage >= 2):
                     continue
                 at = step - 1 if before else step
-                q_step = jnp.maximum(at - 1, 0)
                 if stage == 0:
-                    stage_hidden(g, jnp.minimum(at, steps - 1), q_step)
+                    stage_hidden(g)
                 elif stage == 1:
-                    stage_norm(g, q_step)
+                    stage_norm(g, jnp.maximum(at - 1, 0))
                 elif stage == 2:
                     stage_second(g)
                 else:
                     stage_first(g)
 
+    wait_tokens(0)
+    project(0)
+    wait_tokens(1)
     body(jnp.int32(0), first=True)
 
     def loop_body(step, carry):
+        @pl.when(step < steps - 1)
+        def _():
+            wait_tokens(step + 1)
+
+        @pl.when((step == 7) & (lax.rem(me, 2) == 1))
+        def _():
+            send_far()
+
+        @pl.when(step >= 3)
+        def _():
+            send_out(step - 3)
+
         body(step)
         return carry
 
     lax.fori_loop(1, steps, loop_body, 0)
+    send_out(jnp.int32(steps - 3))
     body(jnp.int32(steps), last=True)
+    send_out(jnp.int32(steps - 2))
     stage_norm(groups - 1, steps - 1)
-
-
-def run_inner(keys, queries, values, w1, w2t, b1, b2, gain, bias, rate):
-    groups, steps = keys.shape[:2]
+    w_keep.wait()
+    w_swap.wait()
+
+    @pl.loop(0, own_steps)
+    def _(chunk):
+        token_copy(0, near, chunk).wait_send()
+        token_copy(1, far_a, chunk).wait_send()
+        token_copy(2, far_b, chunk).wait_send()
+
+    send_out(jnp.int32(steps - 1))
+
+    def out_wait(src, dst, send, recv):
+        return pltpu.make_async_remote_copy(src, dst, send, recv, device_id={'heads': other_row}, device_id_type=mesh_ids)
+
+    def landed(row_at, place):
+        return o_full.at[pl.ds(groups * place, groups), :, pl.ds(width * row_at, width)]
+
+    away = steps - own_steps
+    whole = outs.at[:, pl.ds(0, away)]
+    out_wait(whole, whole, out_send.at[0], out_recv.at[0, 0]).wait_send()
+    out_wait(outs, outs, out_send.at[1], out_recv.at[0, 0]).wait_send()
+    for row_at in range(2):
+        for place in range(parts_of_seq):
+            spot = landed(row_at, place)
+            mine = (row_axis == row_at) & (me == place)
+
+            @pl.when(mine)
+            def _():
+                pltpu.make_async_copy(spot, spot, own_sem).wait()
+
+            @pl.when(jnp.logical_not(mine))
+            def _():
+                out_wait(spot, spot, out_send.at[0], out_recv.at[row_at, place]).wait_recv()
+
+
+def run_layer(tokens, theta_k, theta_q, theta_v, w_out, w1, w2t, b1, b2, gain, bias, rate, parts_of_seq):
+    num_seqs, own_len, model_dim = tokens.shape
+    groups = num_seqs // parts_of_seq
+    steps = own_len * parts_of_seq // MINI_BATCH
     heads = w1.shape[0]
+    width = theta_k.shape[1]
     vmem = pl.BlockSpec(memory_space=pltpu.VMEM)
     smem = pl.BlockSpec(memory_space=pltpu.SMEM)
+    hbm = pl.BlockSpec(memory_space=pl.ANY)
     per_pair = (groups, heads)
     scratch = [((64, 256), f32), ((64, 256), f32), ((192, 256), bf16), ((192, 256), bf16), ((8, 256), f32), ((8, 128), f32),
                ((96, 256), bf16), ((16, 256), f32), ((48, 128), bf16), ((48, 256), bf16), ((48, 128), bf16),
                ((16, 128), f32), ((16, 128), f32), ((16, 128), f32)]
+    scratch = [pltpu.VMEM(per_pair + shape, dtype) for shape, dtype in scratch]
+    scratch += [pltpu.VMEM((heads, 8, 128), f32)] * 2
+    scratch += [pltpu.VMEM((groups, steps, MINI_BATCH, model_dim), bf16), pltpu.VMEM((groups, steps, MINI_BATCH, width), bf16)]
+    scratch += [pltpu.VMEM((groups, MINI_BATCH, width), f32)] * 7
+    own_steps = steps // parts_of_seq
+    dma = pltpu.SemaphoreType.DMA
+    scratch += [dma((3, own_steps)), dma((steps,)), dma((2,)), dma((2, parts_of_seq)), dma, dma, dma, dma]
     return pl.pallas_call(
-        functools.partial(inner_kernel, steps, groups, heads),
-        out_shape=jax.ShapeDtypeStruct(keys.shape, bf16),
-        in_specs=[vmem] * 9 + [smem],
-        out_specs=vmem,
-        scratch_shapes=[pltpu.VMEM(per_pair + shape, dtype) for shape, dtype in scratch],
-        compiler_params=pltpu.CompilerParams(vmem_limit_bytes=60 * 2 ** 20),
-    )(keys, queries, values, w1, w2t, b1, b2, gain, bias, rate)
+        functools.partial(layer_kernel, steps, groups, heads, parts_of_seq),
+        out_shape=(jax.ShapeDtypeStruct((num_seqs, own_len, 2 * width), bf16), jax.ShapeDtypeStruct((2 * width, model_dim), bf16)),
+        in_specs=[hbm] + [vmem] * 3 + [hbm] + [vmem] * 6 + [smem],
+        out_specs=(hbm, hbm),
+        scratch_shapes=scratch,
+        compiler_params=pltpu.CompilerParams(vmem_limit_bytes=60 * 2 ** 20, collective_id=0, has_side_effects=True),
+    )(tokens, theta_k, theta_q, theta_v, w_out, w1, w2t, b1, b2, gain, bias, rate)
 
 
 def solution(mesh):
+    parts_of_seq = mesh.shape['seq']
+
     def local_fn(tokens, theta_q, theta_k, theta_v, w_out, w_one, b_one, w_two, b_two, ln_gain, ln_bias, inner_lr):
-        tok_local, model_dim = tokens.shape[1:]
-        heads = w_one.shape[0]
-        seqs = lax.all_to_all(tokens, 'seq', 0, 1, tiled=True)
-        num_seqs, seq_len = seqs.shape[:2]
-        steps = seq_len // MINI_BATCH
-
-        def project(weight):
-            out = jnp.dot(seqs.reshape(num_seqs * seq_len, model_dim), weight, preferred_element_type=f32)
-            return out.reshape(num_seqs, steps, MINI_BATCH, weight.shape[1])
-
-        def eight(vec, twice):
-            vec = jnp.concatenate([vec, vec], -1) if twice else vec
-            return jnp.broadcast_to(vec[:, None, :], (heads, 8, vec.shape[-1]))
-
-        outs = run_inner(project(theta_k), project(theta_q), project(theta_v), w_one, jnp.swapaxes(w_two, 1, 2), eight(b_one, False),
-                         eight(b_two, True), eight(ln_gain, True), eight(ln_bias, True), inner_lr / MINI_BATCH)
-        outs = outs.reshape(num_seqs, seq_len, outs.shape[-1])
-        outs = lax.all_to_all(outs, 'seq', 1, 0, tiled=True)
-        outs = lax.all_gather(outs, 'heads', axis=2, tiled=True)
-        w_full = lax.all_gather(w_out, 'heads', axis=0, tiled=True)
+        outs, w_full = run_layer(tokens, theta_k, theta_q, theta_v, w_out, w_one, jnp.swapaxes(w_two, 1, 2), b_one, b_two, ln_gain, ln_bias, inner_lr, parts_of_seq)
         return jnp.einsum('bte,ed->btd', outs, w_full, preferred_element_type=f32).astype(bf16)
 
     arg_specs = (P('data', 'seq', None), P(None, 'heads'), P(None, 'heads'), P(None, 'heads'), P('heads', None), P('heads', None, None), P('heads', None), P('heads', None, None), P('heads', None), P('heads', None), P('heads', None), P('heads'))

time: 458 us -> 249 us (0.54)
  waiting for transfers between devices: 182 us -> 0 us
  Pallas kernels: 206 us -> 238 us
  matrix products: 27.2 us -> 11.1 us
  local copies, waits for them, and re-layouts: 14.3 us -> 0 us
  between operations: 13.5 us -> 0.01 us
  starting transfers between devices: 11.6 us -> 0 us
    all_to_all x2 -> x0, waiting for transfers between devices: 101 us -> none  [the longest x1 67 us: local_fn(): seqs = lax.all_to_all(tokens, 'seq', 0, 1, tiled=True)]
    all_gather x2 -> x0, waiting for transfers between devices: 80 us -> none  [the longest x1 79.9 us: local_fn(): outs = lax.all_gather(outs, 'heads', axis=2, tiled=True)]
    pallas_call x1, Pallas kernels: 206 us -> 238 us  [run_layer(): pl.pallas_call(functools.partial(layer_kernel, steps, groups, heads, part...]
    dot_general x3 -> x0, matrix products: 16.1 us -> none  [project(): jnp.dot(seqs.reshape(num_seqs * seq_len, model_dim), weight, preferred_el...]
    all_to_all x2 -> x0, starting transfers between devices: 11.6 us -> none  [the longest x1 6.18 us: local_fn(): outs = lax.all_to_all(outs, 'seq', 1, 0, tiled=True)]
    reshape x1 -> x0, local copies, waits for them, and re-layouts: 5.98 us -> none  [local_fn(): outs = outs.reshape(num_seqs, seq_len, outs.shape[-1])]
    all_to_all x2 -> x0, local copies, waits for them, and re-layouts: 5.86 us -> none  [the longest x1 3.49 us: local_fn(): seqs = lax.all_to_all(tokens, 'seq', 0, 1, tiled=True)]
  transfers between devices with their start and end apart: 4 -> 0, of which waited for: 3 -> 0; matrix products, arithmetic and copies ran while one was open for 1% -> 0% of each run, Pallas kernels for 0% -> 0%
where the time goes in v3:
time: 249 us
  Pallas kernels  238 us (96%)
  matrix products  11.1 us (4%)
    pallas_call x1, Pallas kernels, run_layer(): pl.pallas_call(functools.partial(layer_kernel, steps, groups, heads, part...  238 us
    dot_general x1, matrix products, local_fn(): jnp.einsum('bte,ed->btd', outs, w_full, preferred_element_type=f32)  11.1 us

profile of v3, /device:TPU:3, one launch (start us, length us, event | category | flops | bytes accessed | tf_op | source)
XLA Modules:
  0.0 249.3 jit_solution(4690672289846451175)
XLA Ops:
  0.0 238.2 %shard_map.118 = (bf16[16,192,1024]{2,1,0:T(8,128)(2,1)}, bf16[1024,1024]{1,0:T(8,128)(2,1)}) custom-call(bf16[16,192,1024]{2,1,0:T(8,128)(2,1)} %tokens.1, bf16[1024,512]{1,0:T(8,128)(2,1)} %theta_k.1, bf16[1024,512]{1,0:T(8,128)(2,1)} %theta_q.1, bf16[1024,512]{1,0:T(8,128)(2,1)} %theta_v.1, bf16[512,1024]{1,0:T(8,128)(2,1)} %w_out.1, ...), custom_call_target="tpu_custom_call" | custom-call | tf_op jit(solution)/shard_map/pallas_call | solution.py:354
  238.2 11.1 %convolution_convert_fusion = bf16[16,192,1024]{2,1,0:T(8,128)(2,1)} fusion(bf16[16,192,1024]{2,1,0:T(8,128)(2,1)} %get-tuple-element.7, bf16[1024,1024]{1,0:T(8,128)(2,1)} %get-tuple-element.8), kind=kOutput, calls=%fused_computation | convolution fusion | flops 6445596672 | bytes 14680064 | tf_op jit(solution)/shard_map/bte,ed->btd/dot_general | solution.py:369
